TPU v7x, 512 devices: a whole 4x8x8 slice. The times are simulated.
512 devices in a mesh: shot: 16 (over z, core), pair: 2 (over y_lo), space: 16 (over y_hi, x).
Axes of the slice: x: 4, y: 8 (y_hi: 4, y_lo: 2; y = y_hi * 2 + y_lo), z: 8, core: 2. Of those that a mesh axis runs over, the one named last changes fastest.
Arguments:
- states: float32 [16, 2, 2, 256, 128, 128], P('shot', 'pair', None, 'space'), may hold values from -4 to 4
- courant: float32 [256, 128, 128], P('space'), may hold values from 0.05 to 0.2
- records: float32 [16, 12, 256, 128], P('shot', None, 'space'), may hold values from -6 to 6
Outputs:
- imaging: float32 [256, 128, 128], P('space', 'shot', 'pair')
All inputs are finite; a program needn't handle non-finite values.
Results may differ from a plain program's by a relative error of at most 0.00002.
Values sent between devices are 32-bit elements; how exact they have to be, the bound alone decides.
A program may use at most 64 MiB of HBM per device.

v0:
```python
import jax
import jax.numpy as jnp
from jax import lax
from jax.sharding import PartitionSpec as P

STEPS = 12
IMAGE_EVERY = 2


def extended_2(array, sides, width):
    for axis, dim in sides:
        peers, length = (lax.axis_size(axis), array.shape[dim])
        up = [(i, (i + 1) % peers) for i in range(peers - 1)]
        down = [(j, i) for i, j in up]
        last = lax.slice_in_dim(array, length - width, length, axis=dim)
        first = lax.slice_in_dim(array, 0, width, axis=dim)
        before = lax.ppermute(last, axis, up)
        after = lax.ppermute(first, axis, down)
        array = jnp.concatenate([before, array, after], axis=dim)
    return array


def partner_2(value, axis, distance):
    mask = 2**distance
    pairs = [(source, source ^ mask) for source in range(lax.axis_size(axis))]
    return lax.ppermute(value, axis, pairs)


def split_up(array, dim, peers):
    dims = array.shape
    blocks = array.reshape(*dims[:dim], peers, dims[dim] // peers, *dims[dim + 1 :])
    return jnp.moveaxis(blocks, dim, 0)


def summed_on_arrival(array, axis, dim):
    peers = lax.axis_size(axis)
    blocks = lax.all_to_all(split_up(array, dim, peers), axis, 0, 0, tiled=True)
    return jnp.sum(blocks, axis=0)


def laplacian(extended, center):
    base = center.ndim - 3

    def along(whole, dim_axis, extent):

        def shifted(start):
            return lax.slice_in_dim(whole, start, start + extent, axis=dim_axis)

        return (
            -shifted(0) + 16.0 * shifted(1) - 30.0 * shifted(2) + 16.0 * shifted(3) - shifted(4)
        ) / 12.0

    widths_y = [(0, 0)] * base + [(0, 0), (2, 2), (0, 0)]
    widths_z = [(0, 0)] * base + [(0, 0), (0, 0), (2, 2)]
    total = along(extended, base, center.shape[base])
    total = total + along(jnp.pad(center, widths_y), base + 1, center.shape[base + 1])
    total = total + along(jnp.pad(center, widths_z), base + 2, center.shape[base + 2])
    return total


def on_device(states, courant, records):
    row_role = lax.axis_index("pair")
    inject = (row_role == 1).astype(jnp.float32)
    own_states = states[0, 0]
    rounds = STEPS // IMAGE_EVERY
    weight = IMAGE_EVERY / STEPS
    halfway = courant.shape[2] // 2
    mine_start = row_role * halfway
    other_start = (1 - row_role) * halfway
    blank = jnp.zeros((courant.shape[0], courant.shape[1], halfway), jnp.float32)

    def advance(earlier, current, tick_index):
        extended = extended_2(current, (("space", 0),), 2)
        advanced = 2.0 * current - earlier + courant * laplacian(extended, current)
        record = lax.dynamic_index_in_dim(records[0], tick_index, 0, keepdims=False)
        advanced = advanced.at[:, :, 0].add(inject * record)
        return (current, advanced)

    def one_round(index_round, carry):
        earlier, current, imaging = carry
        for inner in range(IMAGE_EVERY):
            earlier, current = advance(earlier, current, index_round * IMAGE_EVERY + inner)
        outgoing = lax.dynamic_slice_in_dim(current, other_start, halfway, 2)
        partner = partner_2(outgoing, "pair", 0)
        kept = lax.dynamic_slice_in_dim(current, mine_start, halfway, 2)
        return (earlier, current, imaging + kept * partner)

    carry = (own_states[0], own_states[1], blank)
    carry = lax.fori_loop(0, rounds, one_round, carry)
    imaging = carry[2]
    scaled = imaging * weight
    return summed_on_arrival(scaled, "shot", 1)


def solution(mesh):
    placed = (
        P("shot", "pair", None, "space", None, None),
        P("space", None, None),
        P("shot", None, "space", None),
    )
    return jax.shard_map(
        on_device, mesh=mesh, in_specs=placed, out_specs=P("space", "shot", "pair"), check_vma=False
    )
```

profile of v0, /device:TPU:33, one launch (start us, length us, event | category | flops | bytes accessed | tf_op | source)
XLA Modules:
  0.0 388.7 jit_solution(12365774315833858665)
XLA Ops:
  4.5 325.7 %while.22 = (s32[]{:T(128)}, f32[16,128,128]{1,0,2:T(8,128)S(1)}, f32[16,128,128]{1,0,2:T(8,128)S(1)}, f32[16,128,64]{1,0,2:T(8,128)}, f32[16,128,128]{1,0,2:T(8...) while((s32[]{:T(128)}, f32[16,128,128]{1,0,2:T(8,128)S(1)}, ...), condition=%wide.region_1.2_spmd.clone, body=%wide.region_0.1_spmd.clone.sunk | while | flops 17178628 | bytes 21676496 | solution.py:89
  5.3 3.1 collective-permute-start
  8.4 6.4 %collective-permute-start.1 = (f32[2,128,128]{1,0,2:T(2,128)}, f32[2,128,128]{1,0,2:T(2,128)S(1)}, u32[]{:S(2)}, u32[]{:S(2)}) collective-permute-start(f32[2,128,128]{1,0,2:T(2,128)} %get-tuple-element.430), channel_id=1, source_target_pairs={{1,0},{2,1},{3,2},{4,3},{5,4},{6,5},{7,6},{8,7},{9,8},{10,9},{11,1... | collective-permute-start | bytes 393224 | tf_op jit(solution)/shard_map/while/body/eval_jaxpr/ppermute | solution.py:18
  15.9 4.2 %collective-permute-done.1 = f32[2,128,128]{1,0,2:T(2,128)S(1)} collective-permute-done((f32[2,128,128]{1,0,2:T(2,128)}, f32[2,128,128]{1,0,2:T(2,128)S(1)}, u32[]{:S(2)}, u32[]{:S(2)}) %collective-permute-start.1) | collective-permute-done | bytes 131104 | tf_op jit(solution)/shard_map/while/body/eval_jaxpr/ppermute | solution.py:18
  20.9 3.6 fusion.60
  26.0 8.2 %collective-permute-start.2 = (f32[2,128,128]{1,0,2:T(2,128)}, f32[2,128,128]{1,0,2:T(2,128)S(1)}, u32[]{:S(2)}, u32[]{:S(2)}) collective-permute-start(f32[2,128,128]{1,0,2:T(2,128)} %get-tuple-element.431), channel_id=1, source_target_pairs={{1,0},{2,1},{3,2},{4,3},{5,4},{6,5},{7,6},{8,7},{9,8},{10,9},{11,1... | collective-permute-start | bytes 393224 | tf_op jit(solution)/shard_map/while/body/eval_jaxpr/ppermute | solution.py:18
  34.2 1.9 collective-permute-start.3
  36.8 7.7 %collective-permute-done.3 = f32[2,128,128]{1,0,2:T(2,128)S(1)} collective-permute-done((f32[2,128,128]{1,0,2:T(2,128)S(1)}, f32[2,128,128]{1,0,2:T(2,128)S(1)}, u32[]{:S(2)}, u32[]{:S(2)}) %collective-permute-start.3) | collective-permute-done | bytes 131104 | tf_op jit(solution)/shard_map/while/body/eval_jaxpr/ppermute | solution.py:17
  44.5 2.0 fusion.63
  48.0 1.9 collective-permute-start.4
  49.9 11.1 %collective-permute-done.4 = f32[16,128,64]{1,0,2:T(8,128)} collective-permute-done((f32[16,128,64]{1,0,2:T(8,128)}, f32[16,128,64]{1,0,2:T(8,128)}, u32[]{:S(2)}, u32[]{:S(2)}) %collective-permute-start.4) | collective-permute-done | bytes 524320 | tf_op jit(solution)/shard_map/while/body/eval_jaxpr/ppermute | solution.py:26
  61.1 1.9 select_add_fusion.2
  63.7 1.9 collective-permute-start
  65.7 7.6 %collective-permute-start.1 = (f32[2,128,128]{1,0,2:T(2,128)}, f32[2,128,128]{1,0,2:T(2,128)S(1)}, u32[]{:S(2)}, u32[]{:S(2)}) collective-permute-start(f32[2,128,128]{1,0,2:T(2,128)} %get-tuple-element.430), channel_id=1, source_target_pairs={{1,0},{2,1},{3,2},{4,3},{5,4},{6,5},{7,6},{8,7},{9,8},{10,9},{11,1... | collective-permute-start | bytes 393224 | tf_op jit(solution)/shard_map/while/body/eval_jaxpr/ppermute | solution.py:18
  76.6 3.6 fusion.60
  81.7 7.9 %collective-permute-start.2 = (f32[2,128,128]{1,0,2:T(2,128)}, f32[2,128,128]{1,0,2:T(2,128)S(1)}, u32[]{:S(2)}, u32[]{:S(2)}) collective-permute-start(f32[2,128,128]{1,0,2:T(2,128)} %get-tuple-element.431), channel_id=1, source_target_pairs={{1,0},{2,1},{3,2},{4,3},{5,4},{6,5},{7,6},{8,7},{9,8},{10,9},{11,1... | collective-permute-start | bytes 393224 | tf_op jit(solution)/shard_map/while/body/eval_jaxpr/ppermute | solution.py:18
  89.6 1.9 collective-permute-start.3
  91.9 7.6 %collective-permute-done.3 = f32[2,128,128]{1,0,2:T(2,128)S(1)} collective-permute-done((f32[2,128,128]{1,0,2:T(2,128)S(1)}, f32[2,128,128]{1,0,2:T(2,128)S(1)}, u32[]{:S(2)}, u32[]{:S(2)}) %collective-permute-start.3) | collective-permute-done | bytes 131104 | tf_op jit(solution)/shard_map/while/body/eval_jaxpr/ppermute | solution.py:17
  99.5 2.0 fusion.63
  103.0 1.9 collective-permute-start.4
  105.0 8.3 %collective-permute-done.4 = f32[16,128,64]{1,0,2:T(8,128)} collective-permute-done((f32[16,128,64]{1,0,2:T(8,128)}, f32[16,128,64]{1,0,2:T(8,128)}, u32[]{:S(2)}, u32[]{:S(2)}) %collective-permute-start.4) | collective-permute-done | bytes 524320 | tf_op jit(solution)/shard_map/while/body/eval_jaxpr/ppermute | solution.py:26
  113.3 2.1 select_add_fusion.2
  116.1 1.9 collective-permute-start
  118.0 7.6 %collective-permute-start.1 = (f32[2,128,128]{1,0,2:T(2,128)}, f32[2,128,128]{1,0,2:T(2,128)S(1)}, u32[]{:S(2)}, u32[]{:S(2)}) collective-permute-start(f32[2,128,128]{1,0,2:T(2,128)} %get-tuple-element.430), channel_id=1, source_target_pairs={{1,0},{2,1},{3,2},{4,3},{5,4},{6,5},{7,6},{8,7},{9,8},{10,9},{11,1... | collective-permute-start | bytes 393224 | tf_op jit(solution)/shard_map/while/body/eval_jaxpr/ppermute | solution.py:18
  126.7 2.2 collective-permute-done.1
  129.7 3.6 fusion.60
  134.8 7.9 %collective-permute-start.2 = (f32[2,128,128]{1,0,2:T(2,128)}, f32[2,128,128]{1,0,2:T(2,128)S(1)}, u32[]{:S(2)}, u32[]{:S(2)}) collective-permute-start(f32[2,128,128]{1,0,2:T(2,128)} %get-tuple-element.431), channel_id=1, source_target_pairs={{1,0},{2,1},{3,2},{4,3},{5,4},{6,5},{7,6},{8,7},{9,8},{10,9},{11,1... | collective-permute-start | bytes 393224 | tf_op jit(solution)/shard_map/while/body/eval_jaxpr/ppermute | solution.py:18
  142.7 1.9 collective-permute-start.3
  145.0 7.6 %collective-permute-done.3 = f32[2,128,128]{1,0,2:T(2,128)S(1)} collective-permute-done((f32[2,128,128]{1,0,2:T(2,128)S(1)}, f32[2,128,128]{1,0,2:T(2,128)S(1)}, u32[]{:S(2)}, u32[]{:S(2)}) %collective-permute-start.3) | collective-permute-done | bytes 131104 | tf_op jit(solution)/shard_map/while/body/eval_jaxpr/ppermute | solution.py:17
  152.6 2.0 fusion.63
  156.1 1.9 collective-permute-start.4
  158.1 8.3 %collective-permute-done.4 = f32[16,128,64]{1,0,2:T(8,128)} collective-permute-done((f32[16,128,64]{1,0,2:T(8,128)}, f32[16,128,64]{1,0,2:T(8,128)}, u32[]{:S(2)}, u32[]{:S(2)}) %collective-permute-start.4) | collective-permute-done | bytes 524320 | tf_op jit(solution)/shard_map/while/body/eval_jaxpr/ppermute | solution.py:26
  166.4 2.1 select_add_fusion.2
  169.2 1.9 collective-permute-start
  171.1 7.6 %collective-permute-start.1 = (f32[2,128,128]{1,0,2:T(2,128)}, f32[2,128,128]{1,0,2:T(2,128)S(1)}, u32[]{:S(2)}, u32[]{:S(2)}) collective-permute-start(f32[2,128,128]{1,0,2:T(2,128)} %get-tuple-element.430), channel_id=1, source_target_pairs={{1,0},{2,1},{3,2},{4,3},{5,4},{6,5},{7,6},{8,7},{9,8},{10,9},{11,1... | collective-permute-start | bytes 393224 | tf_op jit(solution)/shard_map/while/body/eval_jaxpr/ppermute | solution.py:18
  179.8 2.1 collective-permute-done.1
  182.7 3.6 fusion.60
  187.8 8.0 %collective-permute-start.2 = (f32[2,128,128]{1,0,2:T(2,128)}, f32[2,128,128]{1,0,2:T(2,128)S(1)}, u32[]{:S(2)}, u32[]{:S(2)}) collective-permute-start(f32[2,128,128]{1,0,2:T(2,128)} %get-tuple-element.431), channel_id=1, source_target_pairs={{1,0},{2,1},{3,2},{4,3},{5,4},{6,5},{7,6},{8,7},{9,8},{10,9},{11,1... | collective-permute-start | bytes 393224 | tf_op jit(solution)/shard_map/while/body/eval_jaxpr/ppermute | solution.py:18
  195.8 1.9 collective-permute-start.3
  199.5 6.4 %collective-permute-done.3 = f32[2,128,128]{1,0,2:T(2,128)S(1)} collective-permute-done((f32[2,128,128]{1,0,2:T(2,128)S(1)}, f32[2,128,128]{1,0,2:T(2,128)S(1)}, u32[]{:S(2)}, u32[]{:S(2)}) %collective-permute-start.3) | collective-permute-done | bytes 131104 | tf_op jit(solution)/shard_map/while/body/eval_jaxpr/ppermute | solution.py:17
  205.8 2.0 fusion.63
  209.4 3.5 collective-permute-start.4
  212.9 7.1 %collective-permute-done.4 = f32[16,128,64]{1,0,2:T(8,128)} collective-permute-done((f32[16,128,64]{1,0,2:T(8,128)}, f32[16,128,64]{1,0,2:T(8,128)}, u32[]{:S(2)}, u32[]{:S(2)}) %collective-permute-start.4) | collective-permute-done | bytes 524320 | tf_op jit(solution)/shard_map/while/body/eval_jaxpr/ppermute | solution.py:26
  219.9 2.1 select_add_fusion.2
  224.7 7.6 %collective-permute-start.1 = (f32[2,128,128]{1,0,2:T(2,128)}, f32[2,128,128]{1,0,2:T(2,128)S(1)}, u32[]{:S(2)}, u32[]{:S(2)}) collective-permute-start(f32[2,128,128]{1,0,2:T(2,128)} %get-tuple-element.430), channel_id=1, source_target_pairs={{1,0},{2,1},{3,2},{4,3},{5,4},{6,5},{7,6},{8,7},{9,8},{10,9},{11,1... | collective-permute-start | bytes 393224 | tf_op jit(solution)/shard_map/while/body/eval_jaxpr/ppermute | solution.py:18
  235.3 3.6 fusion.60
  240.4 8.1 %collective-permute-start.2 = (f32[2,128,128]{1,0,2:T(2,128)}, f32[2,128,128]{1,0,2:T(2,128)S(1)}, u32[]{:S(2)}, u32[]{:S(2)}) collective-permute-start(f32[2,128,128]{1,0,2:T(2,128)} %get-tuple-element.431), channel_id=1, source_target_pairs={{1,0},{2,1},{3,2},{4,3},{5,4},{6,5},{7,6},{8,7},{9,8},{10,9},{11,1... | collective-permute-start | bytes 393224 | tf_op jit(solution)/shard_map/while/body/eval_jaxpr/ppermute | solution.py:18
  248.4 1.9 collective-permute-start.3
  250.7 7.7 %collective-permute-done.3 = f32[2,128,128]{1,0,2:T(2,128)S(1)} collective-permute-done((f32[2,128,128]{1,0,2:T(2,128)S(1)}, f32[2,128,128]{1,0,2:T(2,128)S(1)}, u32[]{:S(2)}, u32[]{:S(2)}) %collective-permute-start.3) | collective-permute-done | bytes 131104 | tf_op jit(solution)/shard_map/while/body/eval_jaxpr/ppermute | solution.py:17
  258.4 2.0 fusion.63
  261.9 4.6 %collective-permute-start.4 = (f32[16,128,64]{1,0,2:T(8,128)}, f32[16,128,64]{1,0,2:T(8,128)}, u32[]{:S(2)}, u32[]{:S(2)}) collective-permute-start(f32[16,128,64]{1,0,2:T(8,128)} %constant_dynamic-slice_fusion.2), channel_id=1, source_target_pairs={{0,16},{16,0},{1,17},{17,1},{2,18},{18,2},{3,19},{19,3},{4,20},{20... | collective-permute-start | bytes 1572872 | tf_op jit(solution)/shard_map/while/body/eval_jaxpr/ppermute | solution.py:26
  266.5 8.3 %collective-permute-done.4 = f32[16,128,64]{1,0,2:T(8,128)} collective-permute-done((f32[16,128,64]{1,0,2:T(8,128)}, f32[16,128,64]{1,0,2:T(8,128)}, u32[]{:S(2)}, u32[]{:S(2)}) %collective-permute-start.4) | collective-permute-done | bytes 524320 | tf_op jit(solution)/shard_map/while/body/eval_jaxpr/ppermute | solution.py:26
  274.8 2.1 select_add_fusion.2
  279.5 7.6 %collective-permute-start.1 = (f32[2,128,128]{1,0,2:T(2,128)}, f32[2,128,128]{1,0,2:T(2,128)S(1)}, u32[]{:S(2)}, u32[]{:S(2)}) collective-permute-start(f32[2,128,128]{1,0,2:T(2,128)} %get-tuple-element.430), channel_id=1, source_target_pairs={{1,0},{2,1},{3,2},{4,3},{5,4},{6,5},{7,6},{8,7},{9,8},{10,9},{11,1... | collective-permute-start | bytes 393224 | tf_op jit(solution)/shard_map/while/body/eval_jaxpr/ppermute | solution.py:18
  288.3 2.2 collective-permute-done.1
  291.2 3.6 fusion.60
  296.3 8.0 %collective-permute-start.2 = (f32[2,128,128]{1,0,2:T(2,128)}, f32[2,128,128]{1,0,2:T(2,128)S(1)}, u32[]{:S(2)}, u32[]{:S(2)}) collective-permute-start(f32[2,128,128]{1,0,2:T(2,128)} %get-tuple-element.431), channel_id=1, source_target_pairs={{1,0},{2,1},{3,2},{4,3},{5,4},{6,5},{7,6},{8,7},{9,8},{10,9},{11,1... | collective-permute-start | bytes 393224 | tf_op jit(solution)/shard_map/while/body/eval_jaxpr/ppermute | solution.py:18
  304.3 1.9 collective-permute-start.3
  306.6 7.7 %collective-permute-done.3 = f32[2,128,128]{1,0,2:T(2,128)S(1)} collective-permute-done((f32[2,128,128]{1,0,2:T(2,128)S(1)}, f32[2,128,128]{1,0,2:T(2,128)S(1)}, u32[]{:S(2)}, u32[]{:S(2)}) %collective-permute-start.3) | collective-permute-done | bytes 131104 | tf_op jit(solution)/shard_map/while/body/eval_jaxpr/ppermute | solution.py:17
  314.3 2.0 fusion.63
  317.8 1.9 collective-permute-start.4
  319.7 8.5 %collective-permute-done.4 = f32[16,128,64]{1,0,2:T(8,128)} collective-permute-done((f32[16,128,64]{1,0,2:T(8,128)}, f32[16,128,64]{1,0,2:T(8,128)}, u32[]{:S(2)}, u32[]{:S(2)}) %collective-permute-start.4) | collective-permute-done | bytes 524320 | tf_op jit(solution)/shard_map/while/body/eval_jaxpr/ppermute | solution.py:26
  328.1 2.1 select_add_fusion.2
  332.5 52.7 %all_to_all.5 = f32[16,1,8192]{2,1,0:T(1,128)S(1)} all-to-all(f32[16,1,8192]{2,1,0:T(1,128)S(1)} %reshape.144), channel_id=1, replica_groups=mesh['shot'=16,'pair'=2,'space'=16] {'shot'}, dimensions={0} | all-to-all | bytes 1048576 | tf_op jit(solution)/shard_map/all_to_all | solution.py:37
  (71 shorter events, 53.9 us)
Async XLA Ops:
  5.3 15.6 %collective-permute-start = (f32[2,128,128]{1,0,2:T(2,128)S(1)}, f32[2,128,128]{1,0,2:T(2,128)S(1)}, u32[]{:S(2)}, u32[]{:S(2)}) collective-permute-start(f32[2,128,128]{1,0,2:T(2,128)S(1)} %get-tuple-element.429), channel_id=1, source_target_pairs={{0,1},{1,2},{2,3},{3,4},{4,5},{5,6},{6,7},{7,8},{8,9},{9,10},{10,1... | collective-permute-start | bytes 393224 | tf_op jit(solution)/shard_map/while/body/eval_jaxpr/ppermute | solution.py:17
  8.4 11.8 %collective-permute-start.1 = (f32[2,128,128]{1,0,2:T(2,128)}, f32[2,128,128]{1,0,2:T(2,128)S(1)}, u32[]{:S(2)}, u32[]{:S(2)}) collective-permute-start(f32[2,128,128]{1,0,2:T(2,128)} %get-tuple-element.430), channel_id=1, source_target_pairs={{1,0},{2,1},{3,2},{4,3},{5,4},{6,5},{7,6},{8,7},{9,8},{10,9},{11,1... | collective-permute-start | bytes 393224 | tf_op jit(solution)/shard_map/while/body/eval_jaxpr/ppermute | solution.py:18
  26.0 10.7 %collective-permute-start.2 = (f32[2,128,128]{1,0,2:T(2,128)}, f32[2,128,128]{1,0,2:T(2,128)S(1)}, u32[]{:S(2)}, u32[]{:S(2)}) collective-permute-start(f32[2,128,128]{1,0,2:T(2,128)} %get-tuple-element.431), channel_id=1, source_target_pairs={{1,0},{2,1},{3,2},{4,3},{5,4},{6,5},{7,6},{8,7},{9,8},{10,9},{11,1... | collective-permute-start | bytes 393224 | tf_op jit(solution)/shard_map/while/body/eval_jaxpr/ppermute | solution.py:18
  34.2 10.3 %collective-permute-start.3 = (f32[2,128,128]{1,0,2:T(2,128)S(1)}, f32[2,128,128]{1,0,2:T(2,128)S(1)}, u32[]{:S(2)}, u32[]{:S(2)}) collective-permute-start(f32[2,128,128]{1,0,2:T(2,128)S(1)} %get-tuple-element.432), channel_id=1, source_target_pairs={{0,1},{1,2},{2,3},{3,4},{4,5},{5,6},{6,7},{7,8},{8,9},{9,10},{10,1... | collective-permute-start | bytes 393224 | tf_op jit(solution)/shard_map/while/body/eval_jaxpr/ppermute | solution.py:17
  48.0 13.1 %collective-permute-start.4 = (f32[16,128,64]{1,0,2:T(8,128)}, f32[16,128,64]{1,0,2:T(8,128)}, u32[]{:S(2)}, u32[]{:S(2)}) collective-permute-start(f32[16,128,64]{1,0,2:T(8,128)} %constant_dynamic-slice_fusion.2), channel_id=1, source_target_pairs={{0,16},{16,0},{1,17},{17,1},{2,18},{18,2},{3,19},{19,3},{4,20},{20... | collective-permute-start | bytes 1572872 | tf_op jit(solution)/shard_map/while/body/eval_jaxpr/ppermute | solution.py:26
  63.7 12.8 %collective-permute-start = (f32[2,128,128]{1,0,2:T(2,128)S(1)}, f32[2,128,128]{1,0,2:T(2,128)S(1)}, u32[]{:S(2)}, u32[]{:S(2)}) collective-permute-start(f32[2,128,128]{1,0,2:T(2,128)S(1)} %get-tuple-element.429), channel_id=1, source_target_pairs={{0,1},{1,2},{2,3},{3,4},{4,5},{5,6},{6,7},{7,8},{8,9},{9,10},{10,1... | collective-permute-start | bytes 393224 | tf_op jit(solution)/shard_map/while/body/eval_jaxpr/ppermute | solution.py:17
  65.7 10.2 %collective-permute-start.1 = (f32[2,128,128]{1,0,2:T(2,128)}, f32[2,128,128]{1,0,2:T(2,128)S(1)}, u32[]{:S(2)}, u32[]{:S(2)}) collective-permute-start(f32[2,128,128]{1,0,2:T(2,128)} %get-tuple-element.430), channel_id=1, source_target_pairs={{1,0},{2,1},{3,2},{4,3},{5,4},{6,5},{7,6},{8,7},{9,8},{10,9},{11,1... | collective-permute-start | bytes 393224 | tf_op jit(solution)/shard_map/while/body/eval_jaxpr/ppermute | solution.py:18
  81.7 10.2 %collective-permute-start.2 = (f32[2,128,128]{1,0,2:T(2,128)}, f32[2,128,128]{1,0,2:T(2,128)S(1)}, u32[]{:S(2)}, u32[]{:S(2)}) collective-permute-start(f32[2,128,128]{1,0,2:T(2,128)} %get-tuple-element.431), channel_id=1, source_target_pairs={{1,0},{2,1},{3,2},{4,3},{5,4},{6,5},{7,6},{8,7},{9,8},{10,9},{11,1... | collective-permute-start | bytes 393224 | tf_op jit(solution)/shard_map/while/body/eval_jaxpr/ppermute | solution.py:18
  89.6 9.9 %collective-permute-start.3 = (f32[2,128,128]{1,0,2:T(2,128)S(1)}, f32[2,128,128]{1,0,2:T(2,128)S(1)}, u32[]{:S(2)}, u32[]{:S(2)}) collective-permute-start(f32[2,128,128]{1,0,2:T(2,128)S(1)} %get-tuple-element.432), channel_id=1, source_target_pairs={{0,1},{1,2},{2,3},{3,4},{4,5},{5,6},{6,7},{7,8},{8,9},{9,10},{10,1... | collective-permute-start | bytes 393224 | tf_op jit(solution)/shard_map/while/body/eval_jaxpr/ppermute | solution.py:17
  103.0 10.2 %collective-permute-start.4 = (f32[16,128,64]{1,0,2:T(8,128)}, f32[16,128,64]{1,0,2:T(8,128)}, u32[]{:S(2)}, u32[]{:S(2)}) collective-permute-start(f32[16,128,64]{1,0,2:T(8,128)} %constant_dynamic-slice_fusion.2), channel_id=1, source_target_pairs={{0,16},{16,0},{1,17},{17,1},{2,18},{18,2},{3,19},{19,3},{4,20},{20... | collective-permute-start | bytes 1572872 | tf_op jit(solution)/shard_map/while/body/eval_jaxpr/ppermute | solution.py:26
  116.1 13.6 %collective-permute-start = (f32[2,128,128]{1,0,2:T(2,128)S(1)}, f32[2,128,128]{1,0,2:T(2,128)S(1)}, u32[]{:S(2)}, u32[]{:S(2)}) collective-permute-start(f32[2,128,128]{1,0,2:T(2,128)S(1)} %get-tuple-element.429), channel_id=1, source_target_pairs={{0,1},{1,2},{2,3},{3,4},{4,5},{5,6},{6,7},{7,8},{8,9},{9,10},{10,1... | collective-permute-start | bytes 393224 | tf_op jit(solution)/shard_map/while/body/eval_jaxpr/ppermute | solution.py:17
  118.0 10.9 %collective-permute-start.1 = (f32[2,128,128]{1,0,2:T(2,128)}, f32[2,128,128]{1,0,2:T(2,128)S(1)}, u32[]{:S(2)}, u32[]{:S(2)}) collective-permute-start(f32[2,128,128]{1,0,2:T(2,128)} %get-tuple-element.430), channel_id=1, source_target_pairs={{1,0},{2,1},{3,2},{4,3},{5,4},{6,5},{7,6},{8,7},{9,8},{10,9},{11,1... | collective-permute-start | bytes 393224 | tf_op jit(solution)/shard_map/while/body/eval_jaxpr/ppermute | solution.py:18
  134.8 10.2 %collective-permute-start.2 = (f32[2,128,128]{1,0,2:T(2,128)}, f32[2,128,128]{1,0,2:T(2,128)S(1)}, u32[]{:S(2)}, u32[]{:S(2)}) collective-permute-start(f32[2,128,128]{1,0,2:T(2,128)} %get-tuple-element.431), channel_id=1, source_target_pairs={{1,0},{2,1},{3,2},{4,3},{5,4},{6,5},{7,6},{8,7},{9,8},{10,9},{11,1... | collective-permute-start | bytes 393224 | tf_op jit(solution)/shard_map/while/body/eval_jaxpr/ppermute | solution.py:18
  142.7 9.9 %collective-permute-start.3 = (f32[2,128,128]{1,0,2:T(2,128)S(1)}, f32[2,128,128]{1,0,2:T(2,128)S(1)}, u32[]{:S(2)}, u32[]{:S(2)}) collective-permute-start(f32[2,128,128]{1,0,2:T(2,128)S(1)} %get-tuple-element.432), channel_id=1, source_target_pairs={{0,1},{1,2},{2,3},{3,4},{4,5},{5,6},{6,7},{7,8},{8,9},{9,10},{10,1... | collective-permute-start | bytes 393224 | tf_op jit(solution)/shard_map/while/body/eval_jaxpr/ppermute | solution.py:17
  156.1 10.2 %collective-permute-start.4 = (f32[16,128,64]{1,0,2:T(8,128)}, f32[16,128,64]{1,0,2:T(8,128)}, u32[]{:S(2)}, u32[]{:S(2)}) collective-permute-start(f32[16,128,64]{1,0,2:T(8,128)} %constant_dynamic-slice_fusion.2), channel_id=1, source_target_pairs={{0,16},{16,0},{1,17},{17,1},{2,18},{18,2},{3,19},{19,3},{4,20},{20... | collective-permute-start | bytes 1572872 | tf_op jit(solution)/shard_map/while/body/eval_jaxpr/ppermute | solution.py:26
  169.2 13.5 %collective-permute-start = (f32[2,128,128]{1,0,2:T(2,128)S(1)}, f32[2,128,128]{1,0,2:T(2,128)S(1)}, u32[]{:S(2)}, u32[]{:S(2)}) collective-permute-start(f32[2,128,128]{1,0,2:T(2,128)S(1)} %get-tuple-element.429), channel_id=1, source_target_pairs={{0,1},{1,2},{2,3},{3,4},{4,5},{5,6},{6,7},{7,8},{8,9},{9,10},{10,1... | collective-permute-start | bytes 393224 | tf_op jit(solution)/shard_map/while/body/eval_jaxpr/ppermute | solution.py:17
  171.1 10.8 %collective-permute-start.1 = (f32[2,128,128]{1,0,2:T(2,128)}, f32[2,128,128]{1,0,2:T(2,128)S(1)}, u32[]{:S(2)}, u32[]{:S(2)}) collective-permute-start(f32[2,128,128]{1,0,2:T(2,128)} %get-tuple-element.430), channel_id=1, source_target_pairs={{1,0},{2,1},{3,2},{4,3},{5,4},{6,5},{7,6},{8,7},{9,8},{10,9},{11,1... | collective-permute-start | bytes 393224 | tf_op jit(solution)/shard_map/while/body/eval_jaxpr/ppermute | solution.py:18
  187.8 11.7 %collective-permute-start.2 = (f32[2,128,128]{1,0,2:T(2,128)}, f32[2,128,128]{1,0,2:T(2,128)S(1)}, u32[]{:S(2)}, u32[]{:S(2)}) collective-permute-start(f32[2,128,128]{1,0,2:T(2,128)} %get-tuple-element.431), channel_id=1, source_target_pairs={{1,0},{2,1},{3,2},{4,3},{5,4},{6,5},{7,6},{8,7},{9,8},{10,9},{11,1... | collective-permute-start | bytes 393224 | tf_op jit(solution)/shard_map/while/body/eval_jaxpr/ppermute | solution.py:18
  195.8 10.0 %collective-permute-start.3 = (f32[2,128,128]{1,0,2:T(2,128)S(1)}, f32[2,128,128]{1,0,2:T(2,128)S(1)}, u32[]{:S(2)}, u32[]{:S(2)}) collective-permute-start(f32[2,128,128]{1,0,2:T(2,128)S(1)} %get-tuple-element.432), channel_id=1, source_target_pairs={{0,1},{1,2},{2,3},{3,4},{4,5},{5,6},{6,7},{7,8},{8,9},{9,10},{10,1... | collective-permute-start | bytes 393224 | tf_op jit(solution)/shard_map/while/body/eval_jaxpr/ppermute | solution.py:17
  209.4 10.6 %collective-permute-start.4 = (f32[16,128,64]{1,0,2:T(8,128)}, f32[16,128,64]{1,0,2:T(8,128)}, u32[]{:S(2)}, u32[]{:S(2)}) collective-permute-start(f32[16,128,64]{1,0,2:T(8,128)} %constant_dynamic-slice_fusion.2), channel_id=1, source_target_pairs={{0,16},{16,0},{1,17},{17,1},{2,18},{18,2},{3,19},{19,3},{4,20},{20... | collective-permute-start | bytes 1572872 | tf_op jit(solution)/shard_map/while/body/eval_jaxpr/ppermute | solution.py:26
  222.7 12.5 %collective-permute-start = (f32[2,128,128]{1,0,2:T(2,128)S(1)}, f32[2,128,128]{1,0,2:T(2,128)S(1)}, u32[]{:S(2)}, u32[]{:S(2)}) collective-permute-start(f32[2,128,128]{1,0,2:T(2,128)S(1)} %get-tuple-element.429), channel_id=1, source_target_pairs={{0,1},{1,2},{2,3},{3,4},{4,5},{5,6},{6,7},{7,8},{8,9},{9,10},{10,1... | collective-permute-start | bytes 393224 | tf_op jit(solution)/shard_map/while/body/eval_jaxpr/ppermute | solution.py:17
  224.7 9.9 %collective-permute-start.1 = (f32[2,128,128]{1,0,2:T(2,128)}, f32[2,128,128]{1,0,2:T(2,128)S(1)}, u32[]{:S(2)}, u32[]{:S(2)}) collective-permute-start(f32[2,128,128]{1,0,2:T(2,128)} %get-tuple-element.430), channel_id=1, source_target_pairs={{1,0},{2,1},{3,2},{4,3},{5,4},{6,5},{7,6},{8,7},{9,8},{10,9},{11,1... | collective-permute-start | bytes 393224 | tf_op jit(solution)/shard_map/while/body/eval_jaxpr/ppermute | solution.py:18
  240.4 10.3 %collective-permute-start.2 = (f32[2,128,128]{1,0,2:T(2,128)}, f32[2,128,128]{1,0,2:T(2,128)S(1)}, u32[]{:S(2)}, u32[]{:S(2)}) collective-permute-start(f32[2,128,128]{1,0,2:T(2,128)} %get-tuple-element.431), channel_id=1, source_target_pairs={{1,0},{2,1},{3,2},{4,3},{5,4},{6,5},{7,6},{8,7},{9,8},{10,9},{11,1... | collective-permute-start | bytes 393224 | tf_op jit(solution)/shard_map/while/body/eval_jaxpr/ppermute | solution.py:18
  248.4 9.9 %collective-permute-start.3 = (f32[2,128,128]{1,0,2:T(2,128)S(1)}, f32[2,128,128]{1,0,2:T(2,128)S(1)}, u32[]{:S(2)}, u32[]{:S(2)}) collective-permute-start(f32[2,128,128]{1,0,2:T(2,128)S(1)} %get-tuple-element.432), channel_id=1, source_target_pairs={{0,1},{1,2},{2,3},{3,4},{4,5},{5,6},{6,7},{7,8},{8,9},{9,10},{10,1... | collective-permute-start | bytes 393224 | tf_op jit(solution)/shard_map/while/body/eval_jaxpr/ppermute | solution.py:17
  261.9 12.9 %collective-permute-start.4 = (f32[16,128,64]{1,0,2:T(8,128)}, f32[16,128,64]{1,0,2:T(8,128)}, u32[]{:S(2)}, u32[]{:S(2)}) collective-permute-start(f32[16,128,64]{1,0,2:T(8,128)} %constant_dynamic-slice_fusion.2), channel_id=1, source_target_pairs={{0,16},{16,0},{1,17},{17,1},{2,18},{18,2},{3,19},{19,3},{4,20},{20... | collective-permute-start | bytes 1572872 | tf_op jit(solution)/shard_map/while/body/eval_jaxpr/ppermute | solution.py:26
  277.6 13.6 %collective-permute-start = (f32[2,128,128]{1,0,2:T(2,128)S(1)}, f32[2,128,128]{1,0,2:T(2,128)S(1)}, u32[]{:S(2)}, u32[]{:S(2)}) collective-permute-start(f32[2,128,128]{1,0,2:T(2,128)S(1)} %get-tuple-element.429), channel_id=1, source_target_pairs={{0,1},{1,2},{2,3},{3,4},{4,5},{5,6},{6,7},{7,8},{8,9},{9,10},{10,1... | collective-permute-start | bytes 393224 | tf_op jit(solution)/shard_map/while/body/eval_jaxpr/ppermute | solution.py:17
  279.5 11.0 %collective-permute-start.1 = (f32[2,128,128]{1,0,2:T(2,128)}, f32[2,128,128]{1,0,2:T(2,128)S(1)}, u32[]{:S(2)}, u32[]{:S(2)}) collective-permute-start(f32[2,128,128]{1,0,2:T(2,128)} %get-tuple-element.430), channel_id=1, source_target_pairs={{1,0},{2,1},{3,2},{4,3},{5,4},{6,5},{7,6},{8,7},{9,8},{10,9},{11,1... | collective-permute-start | bytes 393224 | tf_op jit(solution)/shard_map/while/body/eval_jaxpr/ppermute | solution.py:18
  296.3 10.2 %collective-permute-start.2 = (f32[2,128,128]{1,0,2:T(2,128)}, f32[2,128,128]{1,0,2:T(2,128)S(1)}, u32[]{:S(2)}, u32[]{:S(2)}) collective-permute-start(f32[2,128,128]{1,0,2:T(2,128)} %get-tuple-element.431), channel_id=1, source_target_pairs={{1,0},{2,1},{3,2},{4,3},{5,4},{6,5},{7,6},{8,7},{9,8},{10,9},{11,1... | collective-permute-start | bytes 393224 | tf_op jit(solution)/shard_map/while/body/eval_jaxpr/ppermute | solution.py:18
  304.3 9.9 %collective-permute-start.3 = (f32[2,128,128]{1,0,2:T(2,128)S(1)}, f32[2,128,128]{1,0,2:T(2,128)S(1)}, u32[]{:S(2)}, u32[]{:S(2)}) collective-permute-start(f32[2,128,128]{1,0,2:T(2,128)S(1)} %get-tuple-element.432), channel_id=1, source_target_pairs={{0,1},{1,2},{2,3},{3,4},{4,5},{5,6},{6,7},{7,8},{8,9},{9,10},{10,1... | collective-permute-start | bytes 393224 | tf_op jit(solution)/shard_map/while/body/eval_jaxpr/ppermute | solution.py:17
  317.8 10.4 %collective-permute-start.4 = (f32[16,128,64]{1,0,2:T(8,128)}, f32[16,128,64]{1,0,2:T(8,128)}, u32[]{:S(2)}, u32[]{:S(2)}) collective-permute-start(f32[16,128,64]{1,0,2:T(8,128)} %constant_dynamic-slice_fusion.2), channel_id=1, source_target_pairs={{0,16},{16,0},{1,17},{17,1},{2,18},{18,2},{3,19},{19,3},{4,20},{20... | collective-permute-start | bytes 1572872 | tf_op jit(solution)/shard_map/while/body/eval_jaxpr/ppermute | solution.py:26
where the time goes:
time: 390 us; the launch traced here: 389 us
  starting transfers between devices  132 us (34%)
  waiting for transfers between devices  113 us (29%)
  other arithmetic  57.2 us (15%)
  blocking collectives  52.7 us (14%)
  local copies, waits for them, and re-layouts  32.6 us (8%)
    ppermute x12, starting transfers between devices, extended_2(): after = lax.ppermute(first, axis, down)  92.4 us
    all_to_all x1, blocking collectives, summed_on_arrival(): blocks = lax.all_to_all(split_up(array, dim, peers), axis, 0, 0, tiled=True)  52.7 us
    ppermute x6, waiting for transfers between devices, partner_2(): return lax.ppermute(value, axis, pairs)  51.5 us
    ppermute x12, waiting for transfers between devices, extended_2(): before = lax.ppermute(last, axis, up)  44.8 us
    add x12, other arithmetic, advance(): advanced = 2.0 * current - earlier + courant * laplacian(extended, current)  33.7 us
    ppermute x12, starting transfers between devices, extended_2(): before = lax.ppermute(last, axis, up)  24.2 us
    ppermute x12, waiting for transfers between devices, extended_2(): after = lax.ppermute(first, axis, down)  17 us
    ppermute x6, starting transfers between devices, partner_2(): return lax.ppermute(value, axis, pairs)  15.8 us
  transfers between devices with their start and end apart: 30, of which 24 were waited for; matrix products, arithmetic and copies ran while one was open for 3% of the time, Pallas kernels for 0%

commit v1 on v0

v1 whole, which is shorter than its diff:
```python
import functools

import jax
import jax.numpy as jnp
from jax import lax
from jax.experimental import pallas as pl
from jax.experimental.pallas import tpu as pltpu
from jax.sharding import PartitionSpec as P

STEPS = 12
IMAGE_EVERY = 2
ROUNDS = STEPS // IMAGE_EVERY
PAD = 8
DEEP = 4
ROWS = 32
NEAR, FAR, CENTRE = 16.0 / 12.0, 1.0 / 12.0, 90.0 / 12.0


def kernel(
    shots, states, courant, records, out,
    now, old, speed, inject, halo, recs, rec_halo, column,
    kept, arrived, packed, landed,
    load_sem, state_sem, first_sem, speed_sem, rec_sem, rec_halo_sem,
    halo_send, halo_recv, first_send, speed_send, rec_send, rec_halo_send, state_send,
    snap_send, snap_recv, sum_send, sum_recv,
):
    layers, height = states.shape[1], states.shape[2]
    groups = shots // 2
    last_space = lax.axis_size("space") - 1
    shot, pair, space = (lax.axis_index(name) for name in ("shot", "pair", "space"))
    deep, core = shot // 2, lax.rem(shot, 2)
    home_shot = 2 * deep + pair
    moves = core != pair
    has_left, has_right = space > 0, space < last_space
    rows = pl.ds(PAD, height)
    base = DEEP

    def at(shot_at, pair_at, space_at):
        return {"shot": shot_at, "pair": pair_at, "space": space_at}

    def remote(source, target, send, recv, device):
        return pltpu.make_async_remote_copy(
            src_ref=source, dst_ref=target, send_sem=send, recv_sem=recv,
            device_id=device, device_id_type=pl.DeviceIdType.MESH,
        )

    def place(ref, sem):
        return pltpu.make_async_copy(ref, ref, sem)

    mate = at(2 * deep + (1 - core), pair, space)
    home = at(home_shot, core, space)

    barrier = pltpu.get_barrier_semaphore()

    def greet(device):
        pl.semaphore_signal(barrier, inc=1, device_id=device, device_id_type=pl.DeviceIdType.MESH)

    def greet_sides(shot_at, pair_at):
        @pl.when(has_left)
        def _():
            greet(at(shot_at, pair_at, space - 1))

        @pl.when(has_right)
        def _():
            greet(at(shot_at, pair_at, space + 1))

    greet(mate)
    greet_sides(shot, pair)

    @pl.when(moves)
    def _():
        greet(home)
        greet_sides(home_shot, core)

    me = 2 * deep + pair
    for step in range(1, shots):
        peer = lax.rem(me + step, shots)
        greet(at(2 * (peer // 2) + core, lax.rem(peer, 2), space))

    load_speed = pltpu.make_async_copy(courant, speed.at[pl.ds(2, layers)], load_sem.at[0])
    load_speed.start()
    load_old = pltpu.make_async_copy(states.at[0], old.at[pl.ds(base, layers), rows], load_sem.at[1])
    load_now = pltpu.make_async_copy(states.at[1], now.at[pl.ds(base, layers), rows], load_sem.at[2])
    load_recs = pltpu.make_async_copy(records, recs, load_sem.at[3])

    @pl.when(jnp.logical_not(moves))
    def _():
        load_now.start()
        load_old.start()

    @pl.when(core * pair == 1)
    def _():
        load_recs.start()

    zero = jnp.zeros((PAD, now.shape[2]), jnp.float32)

    @pl.loop(0, now.shape[0])
    def _(layer):
        for field in (now, old):
            field[layer, pl.ds(0, PAD)] = zero
            field[layer, pl.ds(PAD + height, PAD)] = zero

    flat = jnp.zeros((height, now.shape[2]), jnp.float32)

    def clear(ref, first, count):
        @pl.loop(0, count)
        def _(layer):
            ref[first + layer, rows] = flat

    @pl.when(jnp.logical_not(has_left))
    def _():
        clear(now, 0, DEEP)
        clear(old, 0, DEEP)
        speed[0] = flat
        speed[1] = flat
        rec_halo[0] = jnp.zeros(rec_halo.shape[1:], jnp.float32)

    @pl.when(jnp.logical_not(has_right))
    def _():
        clear(now, base + layers, DEEP)
        clear(old, base + layers, DEEP)
        speed[layers + 2] = flat
        speed[layers + 3] = flat
        rec_halo[1] = jnp.zeros(rec_halo.shape[1:], jnp.float32)

    column[...] = jnp.zeros(column.shape, jnp.float32)

    sides = jnp.where(has_left, 1, 0) + jnp.where(has_right, 1, 0)
    pl.semaphore_wait(barrier, shots + sides + jnp.where(moves, 1 + sides, 0))

    move_now = remote(states.at[1], now.at[pl.ds(base, layers), rows], state_send.at[0], state_sem.at[0], home)
    move_old = remote(states.at[0], old.at[pl.ds(base, layers), rows], state_send.at[1], state_sem.at[1], home)

    def edges(side):
        there = space - 1 if side == 0 else space + 1
        first4, first2 = (0, 0) if side == 0 else (layers - DEEP, layers - 2)
        far = at(home_shot, core, there)
        near = at(shot, pair, there)
        old_at = base + layers if side == 0 else base - 2
        speed_at = layers + 2 if side == 0 else 0
        return (
            remote(states.at[1, pl.ds(first4, DEEP)], halo.at[0, 1 - side, :, rows],
                   first_send.at[0, side], halo_recv.at[0, 1 - side], far),
            remote(states.at[0, pl.ds(first2, 2)], old.at[pl.ds(old_at, 2), rows],
                   first_send.at[1, side], first_sem.at[1 - side], far),
            remote(courant.at[pl.ds(first2, 2)], speed.at[pl.ds(speed_at, 2)],
                   speed_send.at[side], speed_sem.at[1 - side], near),
        )

    has = (has_left, has_right)
    for side in range(2):
        @pl.when(has[side])
        def _(side=side):
            for copy in edges(side):
                copy.start()

    @pl.when(moves)
    def _():
        move_now.start()
        move_old.start()

    move_recs = remote(records, recs, rec_send, rec_sem, mate)

    @pl.when(core + pair == 0)
    def _():
        move_recs.start()

    @pl.when(core * (1 - pair) == 1)
    def _():
        place(recs, rec_sem).wait()

    @pl.when(core * pair == 1)
    def _():
        load_recs.wait()

    def rec_edge(side):
        there = space - 1 if side == 0 else space + 1
        first = 0 if side == 0 else layers - 8
        return remote(recs.at[:, pl.ds(first, 8)], rec_halo.at[1 - side],
                      rec_halo_send.at[side], rec_halo_sem.at[1 - side], at(shot, pair, there))

    @pl.when(core == 1)
    def _():
        for side in range(2):
            @pl.when(has[side])
            def _(side=side):
                rec_edge(side).start()

        def lay(target, values):
            column[pl.ds(0, STEPS)] = values
            inject[target] = column[...].T

        @pl.loop(0, layers)
        def _(layer):
            lay(2 + layer, recs[:, layer])

        for side in range(2):
            @pl.when(has[side])
            def _(side=side):
                place(rec_halo.at[side], rec_halo_sem.at[side]).wait()

        lay(0, rec_halo[0, :, 6])
        lay(1, rec_halo[0, :, 7])
        lay(layers + 2, rec_halo[1, :, 0])
        lay(layers + 3, rec_halo[1, :, 1])

    @pl.when(core == 0)
    def _():
        @pl.loop(0, layers + 4)
        def _(layer):
            inject[layer] = flat

    width = now.shape[2]
    strip = min(ROWS, height)
    lane = lax.broadcasted_iota(jnp.int32, (strip, width), 1)

    def tick(cur, prev, first, count, index):
        shift = lax.rem(width - index, width)

        @pl.loop(0, count)
        def _(step):
            layer = first + step
            for part in range(0, height, strip):
                here = pl.ds(PAD + part, strip)
                mid = cur[layer, here]
                near = cur[layer - 1, here] + cur[layer + 1, here]
                far = cur[layer - 2, here] + cur[layer + 2, here]
                near += cur[layer, pl.ds(PAD + part - 1, strip)] + cur[layer, pl.ds(PAD + part + 1, strip)]
                far += cur[layer, pl.ds(PAD + part - 2, strip)] + cur[layer, pl.ds(PAD + part + 2, strip)]
                near += jnp.where(lane >= 1, pltpu.roll(mid, 1, 1), 0.0)
                near += jnp.where(lane < width - 1, pltpu.roll(mid, width - 1, 1), 0.0)
                far += jnp.where(lane >= 2, pltpu.roll(mid, 2, 1), 0.0)
                far += jnp.where(lane < width - 2, pltpu.roll(mid, width - 2, 1), 0.0)
                spread = NEAR * near - FAR * far - CENTRE * mid
                at_speed = layer - (base - 2)
                step_to = 2.0 * mid - prev[layer, here] + speed[at_speed, pl.ds(part, strip)] * spread
                added = pltpu.roll(inject[at_speed, pl.ds(part, strip)], shift, 1)
                prev[layer, here] = step_to + jnp.where(lane == 0, added, 0.0)

    load_speed.wait()

    @pl.when(moves)
    def _():
        place(now.at[pl.ds(base, layers), rows], state_sem.at[0]).wait()
        place(old.at[pl.ds(base, layers), rows], state_sem.at[1]).wait()

    @pl.when(jnp.logical_not(moves))
    def _():
        load_now.wait()
        load_old.wait()

    def halo_out(side, slot):
        there = space - 1 if side == 0 else space + 1
        first = base if side == 0 else base + layers - DEEP
        return remote(now.at[pl.ds(first, DEEP), rows], halo.at[slot, 1 - side, :, rows],
                      halo_send.at[side], halo_recv.at[slot, 1 - side], at(shot, pair, there))

    def snapshot(index, group):
        theirs = pl.ds(PAD + 8 * (2 * group + 1 - core), 8)
        return remote(now.at[pl.ds(base, layers), theirs], arrived.at[index, group],
                      snap_send, snap_recv.at[index], mate)

    def snapshot_sent():
        pltpu.make_async_copy(arrived.at[0], arrived.at[0], snap_send).wait()

    @pl.loop(0, ROUNDS)
    def _(turn):
        slot = lax.rem(turn, 2)
        tick(now, old, base + 2, layers - 4, 2 * turn)

        @pl.when(turn > 0)
        def _():
            snapshot_sent()

        tick(old, now, base + 4, layers - 8, 2 * turn + 1)
        for side in range(2):
            edge = 0 if side == 0 else base + layers

            @pl.when(has[side])
            def _(side=side, edge=edge):
                place(halo.at[slot, side, :, rows], halo_recv.at[slot, side]).wait()

                @pl.loop(0, DEEP)
                def _(layer):
                    now[edge + layer, rows] = halo[slot, side, layer, rows]

                @pl.when(turn == 0)
                def _():
                    at_old = base - 2 if side == 0 else base + layers
                    at_speed = 0 if side == 0 else layers + 2
                    place(old.at[pl.ds(at_old, 2), rows], first_sem.at[side]).wait()
                    place(speed.at[pl.ds(at_speed, 2)], speed_sem.at[side]).wait()

                @pl.when(turn > 0)
                def _():
                    halo_out(side, slot).wait_send()

            tick(now, old, base - 2 if side == 0 else base + layers - 2, 4, 2 * turn)
            tick(old, now, base if side == 0 else base + layers - 4, 4, 2 * turn + 1)

            @pl.when(jnp.logical_and(has[side], turn < ROUNDS - 1))
            def _(side=side):
                halo_out(side, 1 - slot).start()

        @pl.loop(0, groups)
        def _(group):
            snapshot(turn, group).start()

        @pl.loop(0, layers)
        def _(layer):
            for group in range(groups):
                mine = pl.ds(pl.multiple_of(PAD + 8 * (2 * group + core), 8), 8)
                kept[turn, group, layer] = now[base + layer, mine]

    half_layers = layers // 2
    low = lax.broadcasted_iota(jnp.int32, (8, width), 1) < width // 2
    for index in range(ROUNDS):
        place(arrived.at[index], snap_recv.at[index]).wait()
    snapshot_sent()

    def picture(group, layer):
        total = kept[0, group, layer] * arrived[0, group, layer]
        for index in range(1, ROUNDS):
            total += kept[index, group, layer] * arrived[index, group, layer]
        return total * (IMAGE_EVERY / STEPS)

    @pl.loop(0, groups)
    def _(group):
        @pl.loop(0, half_layers)
        def _(layer):
            one, two = picture(group, layer), picture(group, half_layers + layer)
            packed[2 * group, layer] = jnp.where(low, one, pltpu.roll(two, width // 2, 1))
            packed[2 * group + 1, layer] = jnp.where(low, pltpu.roll(one, width // 2, 1), two)

    def share(step):
        peer = lax.rem(me + step, shots)
        return remote(packed.at[peer], landed.at[step - 1], sum_send, sum_recv,
                      at(2 * (peer // 2) + core, lax.rem(peer, 2), space))

    @pl.loop(1, shots)
    def _(step):
        share(step).start()

    place(landed, sum_recv).wait()

    @pl.loop(0, half_layers)
    def _(layer):
        total = packed[me, layer]
        for step in range(shots - 1):
            total += landed[step, layer]
        out[layer] = total[:, : width // 2]
        out[half_layers + layer] = pltpu.roll(total, width // 2, 1)[:, : width // 2]

    place(landed, sum_send).wait()
    for side in range(2):
        @pl.when(has[side])
        def _(side=side):
            for copy in edges(side):
                copy.wait_send()

            @pl.when(core == 1)
            def _():
                rec_edge(side).wait_send()

    @pl.when(moves)
    def _():
        move_now.wait_send()
        move_old.wait_send()

    @pl.when(core + pair == 0)
    def _():
        move_recs.wait_send()


def on_device(states, courant, records):
    shots = lax.axis_size("shot")
    layers, height, width = courant.shape
    groups = shots // 2
    dma = pltpu.SemaphoreType.DMA
    field = pltpu.VMEM((layers + 2 * DEEP, height + 2 * PAD, width), jnp.float32)
    extended = pltpu.VMEM((layers + 4, height, width), jnp.float32)
    any_space = pl.BlockSpec(memory_space=pl.ANY)
    return pl.pallas_call(
        functools.partial(kernel, shots),
        out_shape=jax.ShapeDtypeStruct((layers, height // shots, width // 2), jnp.float32),
        in_specs=[any_space] * 3,
        out_specs=pl.BlockSpec(memory_space=pltpu.VMEM),
        scratch_shapes=[
            field, field, extended, extended,
            pltpu.VMEM((2, 2, DEEP, height + 2 * PAD, width), jnp.float32),
            pltpu.VMEM((STEPS, layers, height), jnp.float32),
            pltpu.VMEM((2, STEPS, 8, height), jnp.float32),
            pltpu.VMEM((width, height), jnp.float32),
            pltpu.VMEM((ROUNDS, groups, layers, 8, width), jnp.float32),
            pltpu.VMEM((ROUNDS, groups, layers, 8, width), jnp.float32),
            pltpu.VMEM((shots, layers // 2, 8, width), jnp.float32),
            pltpu.VMEM((shots - 1, layers // 2, 8, width), jnp.float32),
            dma((4,)), dma((2,)), dma((2,)), dma((2,)), dma, dma((2,)),
            dma((2,)), dma((2, 2)), dma((2, 2)), dma((2,)), dma, dma((2,)), dma((2,)),
            dma, dma((ROUNDS,)), dma, dma,
        ],
        compiler_params=pltpu.CompilerParams(
            collective_id=0, has_side_effects=True, vmem_limit_bytes=60 << 20
        ),
    )(states[0, 0], courant, records[0])


def solution(mesh):
    placed = (
        P("shot", "pair", None, "space", None, None),
        P("space", None, None),
        P("shot", None, "space", None),
    )
    return jax.shard_map(
        on_device, mesh=mesh, in_specs=placed, out_specs=P("space", "shot", "pair"), check_vma=False
    )
```

time: 390 us -> 166 us (0.43)
  the two profiles are of different devices: /device:TPU:33 before, /device:TPU:57 now
where the time goes in v1:
time: 166 us
  Pallas kernels  164 us (99%)
    pallas_call x1, Pallas kernels, on_device(): pl.pallas_call(functools.partial(kernel, shots), out_shape=jax.ShapeDtype...  164 us

profile of v1, /device:TPU:57, one launch (start us, length us, event | category | flops | bytes accessed | tf_op | source)
XLA Modules:
  0.0 165.9 jit_solution(11166874949789391343)
XLA Ops:
  0.0 164.5 %shard_map.37 = f32[16,8,64]{2,1,0:T(8,128)} custom-call(f32[2,16,128,128]{3,2,1,0:T(8,128)} %bitcast.2, f32[16,128,128]{2,1,0:T(8,128)} %courant.1, f32[12,16,128]{2,1,0:T(8,128)} %bitcast.3), custom_call_target="tpu_custom_call" | custom-call | tf_op jit(solution)/shard_map/pallas_call | solution.py:383
  164.5 1.5 copy.5

commit v2 on v1

--- a/solution.py
+++ b/solution.py
@@ -1,4 +1,5 @@
 import functools
+import itertools
 
 import jax
 import jax.numpy as jnp
@@ -12,17 +13,19 @@
 ROUNDS = STEPS // IMAGE_EVERY
 PAD = 8
 DEEP = 4
+ROW = 4
 ROWS = 32
 NEAR, FAR, CENTRE = 16.0 / 12.0, 1.0 / 12.0, 90.0 / 12.0
 
 
 def kernel(
     shots, states, courant, records, out,
-    now, old, speed, inject, halo, recs, rec_halo, column,
+    now, old, speed, inject, near_in, far_in, relay_in, recs, rec_halo, column,
     kept, arrived, packed, landed,
-    load_sem, state_sem, first_sem, speed_sem, rec_sem, rec_halo_sem,
-    halo_send, halo_recv, first_send, speed_send, rec_send, rec_halo_send, state_send,
-    snap_send, snap_recv, sum_send, sum_recv,
+    load_sem, state_sem, old_sem, speed_sem, rec_sem, rec_halo_sem,
+    near_send, near_recv, far_send, far_recv, relay_send, relay_recv,
+    first_send, speed_send, hand_send, rec_send, rec_halo_send, state_send,
+    snap_send, snap_recv, inner_send, outer_send, outer_recv, sum_send, sum_recv,
 ):
     layers, height = states.shape[1], states.shape[2]
     groups = shots // 2
@@ -32,6 +35,12 @@
     home_shot = 2 * deep + pair
     moves = core != pair
     has_left, has_right = space > 0, space < last_space
+    has = (has_left, has_right)
+    column_at = lax.rem(space, ROW)
+    at_start, at_end = column_at == 0, column_at == ROW - 1
+    above, below = space + ROW <= last_space, space >= ROW
+    far_end = (jnp.logical_and(at_start, has_left), jnp.logical_and(at_end, has_right))
+    relays = (jnp.logical_and(at_start, above), jnp.logical_and(at_end, below))
     rows = pl.ds(PAD, height)
     base = DEEP
 
@@ -64,13 +73,36 @@
         def _():
             greet(at(shot_at, pair_at, space + 1))
 
+    def greet_rows(shot_at, pair_at):
+        ends = jnp.logical_or(at_start, at_end)
+
+        @pl.when(jnp.logical_and(ends, above))
+        def _():
+            greet(at(shot_at, pair_at, space + ROW))
+
+        @pl.when(jnp.logical_and(ends, below))
+        def _():
+            greet(at(shot_at, pair_at, space - ROW))
+
+    def greet_other_end(shot_at, pair_at):
+        @pl.when(at_start)
+        def _():
+            greet(at(shot_at, pair_at, space + ROW - 1))
+
+        @pl.when(at_end)
+        def _():
+            greet(at(shot_at, pair_at, space - ROW + 1))
+
     greet(mate)
     greet_sides(shot, pair)
+    greet_rows(shot, pair)
+    greet_other_end(shot, pair)
 
     @pl.when(moves)
     def _():
         greet(home)
         greet_sides(home_shot, core)
+        greet_other_end(home_shot, core)
 
     me = 2 * deep + pair
     for step in range(1, shots):
@@ -126,38 +158,72 @@
     column[...] = jnp.zeros(column.shape, jnp.float32)
 
     sides = jnp.where(has_left, 1, 0) + jnp.where(has_right, 1, 0)
-    pl.semaphore_wait(barrier, shots + sides + jnp.where(moves, 1 + sides, 0))
+    ends = jnp.where(jnp.logical_or(at_start, at_end), 1, 0)
+    rows_near = ends * (jnp.where(above, 1, 0) + jnp.where(below, 1, 0))
+    pl.semaphore_wait(
+        barrier, shots + sides + rows_near + ends + jnp.where(moves, 1 + sides + ends, 0)
+    )
 
     move_now = remote(states.at[1], now.at[pl.ds(base, layers), rows], state_send.at[0], state_sem.at[0], home)
     move_old = remote(states.at[0], old.at[pl.ds(base, layers), rows], state_send.at[1], state_sem.at[1], home)
 
-    def edges(side):
+    def split(side, source, target, target_sem, relay, send, shot_at, pair_at, act):
         there = space - 1 if side == 0 else space + 1
-        first4, first2 = (0, 0) if side == 0 else (layers - DEEP, layers - 2)
-        far = at(home_shot, core, there)
-        near = at(shot, pair, there)
-        old_at = base + layers if side == 0 else base - 2
-        speed_at = layers + 2 if side == 0 else 0
-        return (
-            remote(states.at[1, pl.ds(first4, DEEP)], halo.at[0, 1 - side, :, rows],
-                   first_send.at[0, side], halo_recv.at[0, 1 - side], far),
-            remote(states.at[0, pl.ds(first2, 2)], old.at[pl.ds(old_at, 2), rows],
-                   first_send.at[1, side], first_sem.at[1 - side], far),
-            remote(courant.at[pl.ds(first2, 2)], speed.at[pl.ds(speed_at, 2)],
-                   speed_send.at[side], speed_sem.at[1 - side], near),
-        )
-
-    has = (has_left, has_right)
+        over = space + ROW - 1 if side == 0 else space - ROW + 1
+
+        @pl.when(jnp.logical_and(has[side], jnp.logical_not(far_end[side])))
+        def _():
+            act(remote(source, target, send, target_sem, at(shot_at, pair_at, there)))
+
+        @pl.when(far_end[side])
+        def _():
+            act(remote(source, relay_in.at[relay], send, relay_recv.at[relay], at(shot_at, pair_at, over)))
+
+    def old_halo(side):
+        return old.at[pl.ds(base - 2 if side == 0 else base + layers, 2), rows]
+
+    def first_later(side, act):
+        there = space - 1 if side == 0 else space + 1
+
+        @pl.when(has[side])
+        def _():
+            act(remote(states.at[1, pl.ds(0 if side == 0 else layers - 2, 2)], near_in.at[0, 1 - side],
+                       first_send.at[0, side], near_recv.at[0, 1 - side], at(home_shot, core, there)))
+
+        split(side, states.at[1, pl.ds(2 if side == 0 else layers - 4, 2)], far_in.at[0, 1 - side],
+              far_recv.at[0, 1 - side], 0, first_send.at[1, side], home_shot, core, act)
+
+    def first_earlier(side, act):
+        split(side, states.at[0, pl.ds(0 if side == 0 else layers - 2, 2)], old_halo(1 - side), old_sem.at[1 - side],
+              ROUNDS, first_send.at[2, side], home_shot, core, act)
+
+    def speed_halo(side):
+        return speed.at[pl.ds(0 if side == 0 else layers + 2, 2)]
+
+    def speed_edge(side):
+        there = space - 1 if side == 0 else space + 1
+        return remote(courant.at[pl.ds(0 if side == 0 else layers - 2, 2)], speed_halo(1 - side),
+                      speed_send.at[side], speed_sem.at[1 - side], at(shot, pair, there))
+
+    def speed_hand(side):
+        return remote(speed_halo(side), speed_halo(side), hand_send.at[side], speed_sem.at[side], mate)
+
+    stays = jnp.logical_not(moves)
+
     for side in range(2):
-        @pl.when(has[side])
-        def _(side=side):
-            for copy in edges(side):
-                copy.start()
+        first_later(side, lambda copy: copy.start())
 
     @pl.when(moves)
     def _():
         move_now.start()
         move_old.start()
+
+    for side in range(2):
+        first_earlier(side, lambda copy: copy.start())
+
+        @pl.when(jnp.logical_and(has[side], stays))
+        def _(side=side):
+            speed_edge(side).start()
 
     move_recs = remote(records, recs, rec_send, rec_sem, mate)
 
@@ -217,10 +283,10 @@
     def tick(cur, prev, first, count, index):
         shift = lax.rem(width - index, width)
 
-        @pl.loop(0, count)
+        @pl.loop(0, count // 2)
         def _(step):
-            layer = first + step
-            for part in range(0, height, strip):
+            for sub, part in itertools.product(range(2), range(0, height, strip)):
+                layer = first + 2 * step + sub
                 here = pl.ds(PAD + part, strip)
                 mid = cur[layer, here]
                 near = cur[layer - 1, here] + cur[layer + 1, here]
@@ -249,74 +315,54 @@
         load_now.wait()
         load_old.wait()
 
-    def halo_out(side, slot):
+    def near_out(side, turn):
         there = space - 1 if side == 0 else space + 1
-        first = base if side == 0 else base + layers - DEEP
-        return remote(now.at[pl.ds(first, DEEP), rows], halo.at[slot, 1 - side, :, rows],
-                      halo_send.at[side], halo_recv.at[slot, 1 - side], at(shot, pair, there))
-
-    def snapshot(index, group):
-        theirs = pl.ds(PAD + 8 * (2 * group + 1 - core), 8)
-        return remote(now.at[pl.ds(base, layers), theirs], arrived.at[index, group],
-                      snap_send, snap_recv.at[index], mate)
-
-    def snapshot_sent():
-        pltpu.make_async_copy(arrived.at[0], arrived.at[0], snap_send).wait()
-
-    @pl.loop(0, ROUNDS)
-    def _(turn):
-        slot = lax.rem(turn, 2)
-        tick(now, old, base + 2, layers - 4, 2 * turn)
-
-        @pl.when(turn > 0)
-        def _():
-            snapshot_sent()
-
-        tick(old, now, base + 4, layers - 8, 2 * turn + 1)
-        for side in range(2):
-            edge = 0 if side == 0 else base + layers
-
-            @pl.when(has[side])
-            def _(side=side, edge=edge):
-                place(halo.at[slot, side, :, rows], halo_recv.at[slot, side]).wait()
-
-                @pl.loop(0, DEEP)
-                def _(layer):
-                    now[edge + layer, rows] = halo[slot, side, layer, rows]
-
-                @pl.when(turn == 0)
-                def _():
-                    at_old = base - 2 if side == 0 else base + layers
-                    at_speed = 0 if side == 0 else layers + 2
-                    place(old.at[pl.ds(at_old, 2), rows], first_sem.at[side]).wait()
-                    place(speed.at[pl.ds(at_speed, 2)], speed_sem.at[side]).wait()
-
-                @pl.when(turn > 0)
-                def _():
-                    halo_out(side, slot).wait_send()
-
-            tick(now, old, base - 2 if side == 0 else base + layers - 2, 4, 2 * turn)
-            tick(old, now, base if side == 0 else base + layers - 4, 4, 2 * turn + 1)
-
-            @pl.when(jnp.logical_and(has[side], turn < ROUNDS - 1))
-            def _(side=side):
-                halo_out(side, 1 - slot).start()
-
+        edge = base if side == 0 else base + layers - 2
+        return remote(now.at[pl.ds(edge, 2), rows], near_in.at[turn, 1 - side],
+                      near_send.at[side], near_recv.at[turn, 1 - side], at(shot, pair, there))
+
+    def far_out(side, turn, act):
+        edge = base + 2 if side == 0 else base + layers - 4
+        split(side, now.at[pl.ds(edge, 2), rows], far_in.at[turn, 1 - side], far_recv.at[turn, 1 - side], turn,
+              far_send.at[side], shot, pair, act)
+
+    def pass_on(side, turn, act):
+        target = at(shot, pair, space + ROW if side == 0 else space - ROW)
+        act(turn, remote(relay_in.at[turn], far_in.at[turn, side], relay_send.at[turn], far_recv.at[turn, side], target))
+
+        @pl.when(turn == 0)
+        def _():
+            act(ROUNDS, remote(relay_in.at[ROUNDS], old_halo(side), relay_send.at[ROUNDS], old_sem.at[side], target))
+
+    def relay_start(index, copy):
+        place(relay_in.at[index], relay_recv.at[index]).wait()
+        copy.start()
+
+    def take(source, at_layer):
+        for layer in range(2):
+            now[at_layer + layer, rows] = source[layer]
+
+    quarter = layers // 4
+    half = width // 2
+    low = lax.broadcasted_iota(jnp.int32, (8, width), 1) < half
+
+    def snapshot(index, send, recv, spans):
         @pl.loop(0, groups)
         def _(group):
-            snapshot(turn, group).start()
-
-        @pl.loop(0, layers)
-        def _(layer):
-            for group in range(groups):
-                mine = pl.ds(pl.multiple_of(PAD + 8 * (2 * group + core), 8), 8)
-                kept[turn, group, layer] = now[base + layer, mine]
-
-    half_layers = layers // 2
-    low = lax.broadcasted_iota(jnp.int32, (8, width), 1) < width // 2
-    for index in range(ROUNDS):
-        place(arrived.at[index], snap_recv.at[index]).wait()
-    snapshot_sent()
+            theirs = pl.ds(pl.multiple_of(PAD + 8 * (2 * group + 1 - core), 8), 8)
+            for start, count in spans:
+                remote(now.at[pl.ds(base + start, count), theirs], arrived.at[index, group, pl.ds(start, count)],
+                       send, recv, mate).start()
+
+        for start, count in spans:
+            @pl.loop(start, start + count)
+            def _(layer):
+                for group in range(groups):
+                    mine = pl.ds(pl.multiple_of(PAD + 8 * (2 * group + core), 8), 8)
+                    kept[index, group, layer] = now[base + layer, mine]
+
+    def snapshot_sent():
+        place(arrived.at[0], snap_send).wait()
 
     def picture(group, layer):
         total = kept[0, group, layer] * arrived[0, group, layer]
@@ -324,43 +370,143 @@
             total += kept[index, group, layer] * arrived[index, group, layer]
         return total * (IMAGE_EVERY / STEPS)
 
-    @pl.loop(0, groups)
-    def _(group):
-        @pl.loop(0, half_layers)
-        def _(layer):
-            one, two = picture(group, layer), picture(group, half_layers + layer)
-            packed[2 * group, layer] = jnp.where(low, one, pltpu.roll(two, width // 2, 1))
-            packed[2 * group + 1, layer] = jnp.where(low, pltpu.roll(one, width // 2, 1), two)
-
-    def share(step):
+    def share(part, step):
         peer = lax.rem(me + step, shots)
-        return remote(packed.at[peer], landed.at[step - 1], sum_send, sum_recv,
+        return remote(packed.at[part, peer], landed.at[part, step - 1], sum_send.at[part], sum_recv.at[part],
                       at(2 * (peer // 2) + core, lax.rem(peer, 2), space))
 
-    @pl.loop(1, shots)
-    def _(step):
-        share(step).start()
-
-    place(landed, sum_recv).wait()
-
-    @pl.loop(0, half_layers)
-    def _(layer):
-        total = packed[me, layer]
-        for step in range(shots - 1):
-            total += landed[step, layer]
-        out[layer] = total[:, : width // 2]
-        out[half_layers + layer] = pltpu.roll(total, width // 2, 1)[:, : width // 2]
-
-    place(landed, sum_send).wait()
+    def send_image(part):
+        one_at, two_at = (quarter, 2 * quarter) if part == 0 else (0, 3 * quarter)
+
+        @pl.loop(0, groups)
+        def _(group):
+            for q in range(quarter):
+                one, two = picture(group, one_at + q), picture(group, two_at + q)
+                packed[part, 2 * group, q] = jnp.where(low, one, pltpu.roll(two, half, 1))
+                packed[part, 2 * group + 1, q] = jnp.where(low, pltpu.roll(one, half, 1), two)
+
+        @pl.loop(1, shots)
+        def _(step):
+            share(part, step).start()
+
+    def take_image(part):
+        one_at, two_at = (quarter, 2 * quarter) if part == 0 else (0, 3 * quarter)
+        place(landed.at[part], sum_recv.at[part]).wait()
+        for q in range(quarter):
+            total = packed[part, me, q]
+            for step in range(shots - 1):
+                total += landed[part, step, q]
+            out[one_at + q] = total[:, :half]
+            out[two_at + q] = pltpu.roll(total, half, 1)[:, :half]
+
+    last = ROUNDS - 1
+    inner_rows = arrived.at[last, :, pl.ds(quarter, 2 * quarter)]
+
+    @pl.loop(0, ROUNDS)
+    def _(turn):
+        even, odd = 2 * turn, 2 * turn + 1
+        tick(now, old, base + 2, layers - 4, even)
+
+        @pl.when(turn > 0)
+        def _():
+            snapshot_sent()
+
+        tick(old, now, base + 4, layers - 8, odd)
+
+        @pl.when(turn == last)
+        def _():
+            snapshot(last, inner_send, snap_recv.at[last], ((quarter, 2 * quarter),))
+
+        for side in range(2):
+            @pl.when(relays[side])
+            def _(side=side):
+                pass_on(side, turn, relay_start)
+
+        @pl.when(turn == last)
+        def _():
+            for index in range(last):
+                place(arrived.at[index], snap_recv.at[index]).wait()
+            place(inner_rows, snap_recv.at[last]).wait()
+            send_image(0)
+
+        for side in range(2):
+            @pl.when(has[side])
+            def _(side=side):
+                place(near_in.at[turn, side], near_recv.at[turn, side]).wait()
+                take(near_in.at[turn, side], base - 2 if side == 0 else base + layers)
+
+            @pl.when(turn > 0)
+            def _(side=side):
+                far_out(side, turn, lambda copy: copy.wait_send())
+
+            tick(now, old, base if side == 0 else base + layers - 2, 2, even)
+            tick(old, now, base + 2 if side == 0 else base + layers - 4, 2, odd)
+
+            @pl.when(turn < ROUNDS - 1)
+            def _(side=side):
+                far_out(side, turn + 1, lambda copy: copy.start())
+
+        for side in range(2):
+            @pl.when(has[side])
+            def _(side=side):
+                place(far_in.at[turn, side], far_recv.at[turn, side]).wait()
+                take(far_in.at[turn, side], base - 4 if side == 0 else base + layers + 2)
+
+                @pl.when(turn == 0)
+                def _():
+                    place(old_halo(side), old_sem.at[side]).wait()
+                    place(speed_halo(side), speed_sem.at[side]).wait()
+
+                    @pl.when(stays)
+                    def _():
+                        speed_hand(side).start()
+
+                @pl.when(turn > 0)
+                def _():
+                    near_out(side, turn).wait_send()
+
+            tick(now, old, base - 2 if side == 0 else base + layers, 2, even)
+            tick(old, now, base if side == 0 else base + layers - 2, 2, odd)
+
+            @pl.when(jnp.logical_and(has[side], turn < ROUNDS - 1))
+            def _(side=side):
+                near_out(side, turn + 1).start()
+
+        @pl.when(turn < last)
+        def _():
+            snapshot(turn, snap_send, snap_recv.at[turn], ((0, layers),))
+
+        @pl.when(turn == last)
+        def _():
+            snapshot(last, outer_send, outer_recv, ((0, quarter), (3 * quarter, quarter)))
+
+    place(inner_rows, outer_recv).wait()
+    send_image(1)
+    take_image(0)
+    take_image(1)
+
+    for part in range(2):
+        place(landed.at[part], sum_send.at[part]).wait()
+    place(inner_rows, inner_send).wait()
+    place(inner_rows, outer_send).wait()
     for side in range(2):
-        @pl.when(has[side])
+        first_later(side, lambda copy: copy.wait_send())
+        first_earlier(side, lambda copy: copy.wait_send())
+
+        @pl.when(jnp.logical_and(has[side], stays))
         def _(side=side):
-            for copy in edges(side):
-                copy.wait_send()
-
-            @pl.when(core == 1)
-            def _():
-                rec_edge(side).wait_send()
+            speed_edge(side).wait_send()
+            speed_hand(side).wait_send()
+
+        @pl.when(jnp.logical_and(has[side], core == 1))
+        def _(side=side):
+            rec_edge(side).wait_send()
+
+        @pl.when(relays[side])
+        def _(side=side):
+            @pl.loop(0, ROUNDS)
+            def _(turn):
+                pass_on(side, turn, lambda index, copy: copy.wait_send())
 
     @pl.when(moves)
     def _():
@@ -387,17 +533,20 @@
         out_specs=pl.BlockSpec(memory_space=pltpu.VMEM),
         scratch_shapes=[
             field, field, extended, extended,
-            pltpu.VMEM((2, 2, DEEP, height + 2 * PAD, width), jnp.float32),
+            pltpu.VMEM((ROUNDS, 2, 2, height, width), jnp.float32),
+            pltpu.VMEM((ROUNDS, 2, 2, height, width), jnp.float32),
+            pltpu.VMEM((ROUNDS + 1, 2, height, width), jnp.float32),
             pltpu.VMEM((STEPS, layers, height), jnp.float32),
             pltpu.VMEM((2, STEPS, 8, height), jnp.float32),
             pltpu.VMEM((width, height), jnp.float32),
             pltpu.VMEM((ROUNDS, groups, layers, 8, width), jnp.float32),
             pltpu.VMEM((ROUNDS, groups, layers, 8, width), jnp.float32),
-            pltpu.VMEM((shots, layers // 2, 8, width), jnp.float32),
-            pltpu.VMEM((shots - 1, layers // 2, 8, width), jnp.float32),
+            pltpu.VMEM((2, shots, layers // 4, 8, width), jnp.float32),
+            pltpu.VMEM((2, shots - 1, layers // 4, 8, width), jnp.float32),
             dma((4,)), dma((2,)), dma((2,)), dma((2,)), dma, dma((2,)),
-            dma((2,)), dma((2, 2)), dma((2, 2)), dma((2,)), dma, dma((2,)), dma((2,)),
-            dma, dma((ROUNDS,)), dma, dma,
+            dma((2,)), dma((ROUNDS, 2)), dma((2,)), dma((ROUNDS, 2)), dma((ROUNDS + 1,)), dma((ROUNDS + 1,)),
+            dma((3, 2)), dma((2,)), dma((2,)), dma, dma((2,)), dma((2,)),
+            dma, dma((ROUNDS,)), dma, dma, dma, dma((2,)), dma((2,)),
         ],
         compiler_params=pltpu.CompilerParams(
             collective_id=0, has_side_effects=True, vmem_limit_bytes=60 << 20

time: 166 us -> 129 us (0.78); the launches traced: 166 us -> 126 us
  Pallas kernels: 164 us -> 125 us
    pallas_call x1, Pallas kernels: 164 us -> 125 us  [on_device(): pl.pallas_call(functools.partial(kernel, shots), out_shape=jax.ShapeDtype...]
where the time goes in v2:
time: 129 us; the launch traced here: 126 us
  Pallas kernels  125 us (97%)
  local copies, waits for them, and re-layouts  1.47 us (1%)
    pallas_call x1, Pallas kernels, on_device(): pl.pallas_call(functools.partial(kernel, shots), out_shape=jax.ShapeDtype...  125 us

profile of v2, /device:TPU:57, one launch (start us, length us, event | category | flops | bytes accessed | tf_op | source)
XLA Modules:
  0.0 126.4 jit_solution(15011339099139762942)
XLA Ops:
  0.0 124.9 %shard_map.37 = f32[16,8,64]{2,1,0:T(8,128)} custom-call(f32[2,16,128,128]{3,2,1,0:T(8,128)} %bitcast.2, f32[16,128,128]{2,1,0:T(8,128)} %courant.1, f32[12,16,128]{2,1,0:T(8,128)} %bitcast.3), custom_call_target="tpu_custom_call" | custom-call | tf_op jit(solution)/shard_map/pallas_call | solution.py:529
  124.9 1.5 %copy.5 = f32[16,8,64]{2,1,0:T(8,128)} copy(f32[16,8,64]{2,1,0:T(8,128)} %shard_map.37) | data formatting | bytes 65536

commit v3 on v2

--- a/solution.py
+++ b/solution.py
@@ -25,7 +25,7 @@
     load_sem, state_sem, old_sem, speed_sem, rec_sem, rec_halo_sem,
     near_send, near_recv, far_send, far_recv, relay_send, relay_recv,
     first_send, speed_send, hand_send, rec_send, rec_halo_send, state_send,
-    snap_send, snap_recv, inner_send, outer_send, outer_recv, sum_send, sum_recv,
+    snap_send, snap_recv, inner_send, outer_send, outer_recv, sum_send, sum_recv, clear_road,
 ):
     layers, height = states.shape[1], states.shape[2]
     groups = shots // 2
@@ -56,6 +56,12 @@
     def place(ref, sem):
         return pltpu.make_async_copy(ref, ref, sem)
 
+    def begin(copy):
+        copy.start()
+
+    def sent(copy):
+        copy.wait_send()
+
     mate = at(2 * deep + (1 - core), pair, space)
     home = at(home_shot, core, space)
 
@@ -167,6 +173,14 @@
     move_now = remote(states.at[1], now.at[pl.ds(base, layers), rows], state_send.at[0], state_sem.at[0], home)
     move_old = remote(states.at[0], old.at[pl.ds(base, layers), rows], state_send.at[1], state_sem.at[1], home)
 
+    def by_layer(act, source, target, send, recv, device):
+        if act is begin:
+            for layer in range(2):
+                one = pl.ds(layer, 1)
+                remote(source.at[one], target.at[one], send, recv.at[layer], device).start()
+        else:
+            act(remote(source, target, send, recv.at[0], device))
+
     def split(side, source, target, target_sem, relay, send, shot_at, pair_at, act):
         there = space - 1 if side == 0 else space + 1
         over = space + ROW - 1 if side == 0 else space - ROW + 1
@@ -177,7 +191,7 @@
 
         @pl.when(far_end[side])
         def _():
-            act(remote(source, relay_in.at[relay], send, relay_recv.at[relay], at(shot_at, pair_at, over)))
+            by_layer(act, source, relay_in.at[relay], send, relay_recv.at[relay], at(shot_at, pair_at, over))
 
     def old_halo(side):
         return old.at[pl.ds(base - 2 if side == 0 else base + layers, 2), rows]
@@ -211,7 +225,7 @@
     stays = jnp.logical_not(moves)
 
     for side in range(2):
-        first_later(side, lambda copy: copy.start())
+        first_later(side, begin)
 
     @pl.when(moves)
     def _():
@@ -219,7 +233,7 @@
         move_old.start()
 
     for side in range(2):
-        first_earlier(side, lambda copy: copy.start())
+        first_earlier(side, begin)
 
         @pl.when(jnp.logical_and(has[side], stays))
         def _(side=side):
@@ -303,18 +317,6 @@
                 added = pltpu.roll(inject[at_speed, pl.ds(part, strip)], shift, 1)
                 prev[layer, here] = step_to + jnp.where(lane == 0, added, 0.0)
 
-    load_speed.wait()
-
-    @pl.when(moves)
-    def _():
-        place(now.at[pl.ds(base, layers), rows], state_sem.at[0]).wait()
-        place(old.at[pl.ds(base, layers), rows], state_sem.at[1]).wait()
-
-    @pl.when(jnp.logical_not(moves))
-    def _():
-        load_now.wait()
-        load_old.wait()
-
     def near_out(side, turn):
         there = space - 1 if side == 0 else space + 1
         edge = base if side == 0 else base + layers - 2
@@ -326,23 +328,41 @@
         split(side, now.at[pl.ds(edge, 2), rows], far_in.at[turn, 1 - side], far_recv.at[turn, 1 - side], turn,
               far_send.at[side], shot, pair, act)
 
-    def pass_on(side, turn, act):
-        target = at(shot, pair, space + ROW if side == 0 else space - ROW)
-        act(turn, remote(relay_in.at[turn], far_in.at[turn, side], relay_send.at[turn], far_recv.at[turn, side], target))
-
-        @pl.when(turn == 0)
-        def _():
-            act(ROUNDS, remote(relay_in.at[ROUNDS], old_halo(side), relay_send.at[ROUNDS], old_sem.at[side], target))
-
-    def relay_start(index, copy):
-        place(relay_in.at[index], relay_recv.at[index]).wait()
-        copy.start()
+    def relay_target(side):
+        return at(shot, pair, space + ROW if side == 0 else space - ROW)
+
+    def forward(index, target, recv, side):
+        for layer in range(2):
+            one = pl.ds(layer, 1)
+            place(relay_in.at[index, one], relay_recv.at[index, layer]).wait()
+            remote(relay_in.at[index, one], target.at[one], relay_send.at[index], recv, relay_target(side)).start()
+
+    def pass_on(side, turn):
+        forward(turn, far_in.at[turn, side], far_recv.at[turn, side], side)
+
+    for side in range(2):
+        @pl.when(relays[side])
+        def _(side=side):
+            pass_on(side, 0)
+            forward(ROUNDS, old_halo(side), old_sem.at[side], side)
+
+    load_speed.wait()
+
+    @pl.when(moves)
+    def _():
+        place(now.at[pl.ds(base, layers), rows], state_sem.at[0]).wait()
+        place(old.at[pl.ds(base, layers), rows], state_sem.at[1]).wait()
+        pl.semaphore_signal(clear_road, inc=1, device_id=mate, device_id_type=pl.DeviceIdType.MESH)
+
+    @pl.when(jnp.logical_not(moves))
+    def _():
+        load_now.wait()
+        load_old.wait()
 
     def take(source, at_layer):
         for layer in range(2):
             now[at_layer + layer, rows] = source[layer]
 
-    quarter = layers // 4
     half = width // 2
     low = lax.broadcasted_iota(jnp.int32, (8, width), 1) < half
 
@@ -376,11 +396,11 @@
                       at(2 * (peer // 2) + core, lax.rem(peer, 2), space))
 
     def send_image(part):
-        one_at, two_at = (quarter, 2 * quarter) if part == 0 else (0, 3 * quarter)
+        one_at, two_at = pairs_at[part]
 
         @pl.loop(0, groups)
         def _(group):
-            for q in range(quarter):
+            for q in range(2):
                 one, two = picture(group, one_at + q), picture(group, two_at + q)
                 packed[part, 2 * group, q] = jnp.where(low, one, pltpu.roll(two, half, 1))
                 packed[part, 2 * group + 1, q] = jnp.where(low, pltpu.roll(one, half, 1), two)
@@ -390,9 +410,9 @@
             share(part, step).start()
 
     def take_image(part):
-        one_at, two_at = (quarter, 2 * quarter) if part == 0 else (0, 3 * quarter)
+        one_at, two_at = pairs_at[part]
         place(landed.at[part], sum_recv.at[part]).wait()
-        for q in range(quarter):
+        for q in range(2):
             total = packed[part, me, q]
             for step in range(shots - 1):
                 total += landed[part, step, q]
@@ -400,7 +420,9 @@
             out[two_at + q] = pltpu.roll(total, half, 1)[:, :half]
 
     last = ROUNDS - 1
-    inner_rows = arrived.at[last, :, pl.ds(quarter, 2 * quarter)]
+    pairs_at = ((4, layers - 8), (6, layers - 6), (2, layers - 4), (0, layers - 2))
+    inner_rows = arrived.at[last, :, pl.ds(4, layers - 8)]
+    outer_rows = arrived.at[last, :, pl.ds(0, 4)]
 
     @pl.loop(0, ROUNDS)
     def _(turn):
@@ -415,12 +437,7 @@
 
         @pl.when(turn == last)
         def _():
-            snapshot(last, inner_send, snap_recv.at[last], ((quarter, 2 * quarter),))
-
-        for side in range(2):
-            @pl.when(relays[side])
-            def _(side=side):
-                pass_on(side, turn, relay_start)
+            snapshot(last, inner_send, snap_recv.at[last], ((4, layers - 8),))
 
         @pl.when(turn == last)
         def _():
@@ -428,6 +445,11 @@
                 place(arrived.at[index], snap_recv.at[index]).wait()
             place(inner_rows, snap_recv.at[last]).wait()
             send_image(0)
+            send_image(1)
+
+        @pl.when(jnp.logical_and(turn == 0, stays))
+        def _():
+            pl.semaphore_wait(clear_road, 1)
 
         for side in range(2):
             @pl.when(has[side])
@@ -437,14 +459,20 @@
 
             @pl.when(turn > 0)
             def _(side=side):
-                far_out(side, turn, lambda copy: copy.wait_send())
+                far_out(side, turn, sent)
 
             tick(now, old, base if side == 0 else base + layers - 2, 2, even)
             tick(old, now, base + 2 if side == 0 else base + layers - 4, 2, odd)
 
             @pl.when(turn < ROUNDS - 1)
             def _(side=side):
-                far_out(side, turn + 1, lambda copy: copy.start())
+                far_out(side, turn + 1, begin)
+
+        @pl.when(turn == last)
+        def _():
+            snapshot(last, outer_send.at[0], outer_recv.at[0], ((2, 2), (layers - 4, 2)))
+            place(outer_rows, outer_recv.at[0]).wait()
+            send_image(2)
 
         for side in range(2):
             @pl.when(has[side])
@@ -472,26 +500,32 @@
             def _(side=side):
                 near_out(side, turn + 1).start()
 
+        for side in range(2):
+            @pl.when(jnp.logical_and(relays[side], turn < last))
+            def _(side=side):
+                pass_on(side, turn + 1)
+
         @pl.when(turn < last)
         def _():
             snapshot(turn, snap_send, snap_recv.at[turn], ((0, layers),))
 
         @pl.when(turn == last)
         def _():
-            snapshot(last, outer_send, outer_recv, ((0, quarter), (3 * quarter, quarter)))
-
-    place(inner_rows, outer_recv).wait()
-    send_image(1)
-    take_image(0)
-    take_image(1)
-
-    for part in range(2):
+            snapshot(last, outer_send.at[1], outer_recv.at[1], ((0, 2), (layers - 2, 2)))
+
+    place(outer_rows, outer_recv.at[1]).wait()
+    send_image(3)
+    for part in range(4):
+        take_image(part)
+
+    for part in range(4):
         place(landed.at[part], sum_send.at[part]).wait()
     place(inner_rows, inner_send).wait()
-    place(inner_rows, outer_send).wait()
+    for index in range(2):
+        place(outer_rows, outer_send.at[index]).wait()
     for side in range(2):
-        first_later(side, lambda copy: copy.wait_send())
-        first_earlier(side, lambda copy: copy.wait_send())
+        first_later(side, sent)
+        first_earlier(side, sent)
 
         @pl.when(jnp.logical_and(has[side], stays))
         def _(side=side):
@@ -504,9 +538,9 @@
 
         @pl.when(relays[side])
         def _(side=side):
-            @pl.loop(0, ROUNDS)
-            def _(turn):
-                pass_on(side, turn, lambda index, copy: copy.wait_send())
+            @pl.loop(0, ROUNDS + 1)
+            def _(index):
+                place(relay_in.at[index], relay_send.at[index]).wait()
 
     @pl.when(moves)
     def _():
@@ -541,12 +575,13 @@
             pltpu.VMEM((width, height), jnp.float32),
             pltpu.VMEM((ROUNDS, groups, layers, 8, width), jnp.float32),
             pltpu.VMEM((ROUNDS, groups, layers, 8, width), jnp.float32),
-            pltpu.VMEM((2, shots, layers // 4, 8, width), jnp.float32),
-            pltpu.VMEM((2, shots - 1, layers // 4, 8, width), jnp.float32),
+            pltpu.VMEM((4, shots, 2, 8, width), jnp.float32),
+            pltpu.VMEM((4, shots - 1, 2, 8, width), jnp.float32),
             dma((4,)), dma((2,)), dma((2,)), dma((2,)), dma, dma((2,)),
-            dma((2,)), dma((ROUNDS, 2)), dma((2,)), dma((ROUNDS, 2)), dma((ROUNDS + 1,)), dma((ROUNDS + 1,)),
+            dma((2,)), dma((ROUNDS, 2)), dma((2,)), dma((ROUNDS, 2)), dma((ROUNDS + 1,)), dma((ROUNDS + 1, 2)),
             dma((3, 2)), dma((2,)), dma((2,)), dma, dma((2,)), dma((2,)),
-            dma, dma((ROUNDS,)), dma, dma, dma, dma((2,)), dma((2,)),
+            dma, dma((ROUNDS,)), dma, dma((2,)), dma((2,)), dma((4,)), dma((4,)),
+            pltpu.SemaphoreType.REGULAR,
         ],
         compiler_params=pltpu.CompilerParams(
             collective_id=0, has_side_effects=True, vmem_limit_bytes=60 << 20

time: 129 us -> 128 us (level)
  the two profiles are of different devices: /device:TPU:57 before, /device:TPU:46 now
where the time goes in v3:
time: 128 us; the launch traced here: 127 us
  Pallas kernels  126 us (98%)
  local copies, waits for them, and re-layouts  1.47 us (1%)
    pallas_call x1, Pallas kernels, on_device(): pl.pallas_call(functools.partial(kernel, shots), out_shape=jax.ShapeDtype...  126 us

profile of v3, /device:TPU:46, one launch (start us, length us, event | category | flops | bytes accessed | tf_op | source)
XLA Modules:
  0.0 127.4 jit_solution(8840783964042032427)
XLA Ops:
  0.0 125.9 %shard_map.37 = f32[16,8,64]{2,1,0:T(8,128)} custom-call(f32[2,16,128,128]{3,2,1,0:T(8,128)} %bitcast.2, f32[16,128,128]{2,1,0:T(8,128)} %courant.1, f32[12,16,128]{2,1,0:T(8,128)} %bitcast.3), custom_call_target="tpu_custom_call" | custom-call | tf_op jit(solution)/shard_map/pallas_call | solution.py:563
  125.9 1.5 %copy.5 = f32[16,8,64]{2,1,0:T(8,128)} copy(f32[16,8,64]{2,1,0:T(8,128)} %shard_map.37) | data formatting | bytes 65536
